TPU v7x, 32 devices: a whole 2x2x4 slice. The times are simulated.
32 devices in a mesh: seq: 16 (over z, y, x), blk: 2 (over core).
Axes of the slice: x: 2, y: 2, z: 4, core: 2. Of those that a mesh axis runs over, the one named last changes fastest.
Arguments:
- query: bfloat16 [2048, 5120], P(('blk', 'seq')), may hold values from -139 to 139
- keys: bfloat16 [2048, 5120], P(('blk', 'seq')), may hold values from -4.5 to 4.5
- values: bfloat16 [2048, 5120], P(('blk', 'seq')), may hold values from -6 to 6
Outputs:
- attended: bfloat16 [2048, 5120], P(('blk', 'seq'))
All inputs are finite; a program needn't handle non-finite values.
Results may differ from a plain program's by a relative error of at most 0.008.
Values may be sent and summed in bfloat16 or wider, within the bound.
No kernel may reach another device: no remote copies, remote signals or barrier semaphores. Data moves between devices by JAX's collectives and lax.ppermute only.
A program may use at most 64 MiB of HBM per device.

v0:
```python
import jax
import jax.numpy as jnp
from jax import lax
from jax.sharding import PartitionSpec as P

HEADS = 40


def partner(value, axis, bit):
    mask = 2**bit
    pairs = [(source, source ^ mask) for source in range(lax.axis_size(axis))]
    return lax.ppermute(value, axis, pairs)


def partial_block(q_rows, k_tile, v_tile):
    scores = lax.dot_general(
        q_rows, k_tile, (((1,), (1,)), ((), ())), preferred_element_type=jnp.float32
    ) * q_rows.shape[1] ** (-0.5)
    peak = jnp.max(scores, axis=1)
    expo = jnp.exp(scores - peak[:, None])
    totals = jnp.sum(expo, axis=1)
    summed = jnp.dot(expo.astype(jnp.bfloat16), v_tile, preferred_element_type=jnp.float32)
    return (peak, totals, summed)


def combine_parts(left, right):
    peak = jnp.maximum(left[0], right[0])
    scale_left = jnp.exp(left[0] - peak)
    scale_right = jnp.exp(right[0] - peak)
    totals = scale_left * left[1] + scale_right * right[1]
    summed = scale_left[:, None] * left[2] + scale_right[:, None] * right[2]
    return (peak, totals, summed)


def attend_rows(q_rows, first_k, first_v, second_k, second_v):
    state = partial_block(q_rows, first_k, first_v)
    state = combine_parts(state, partial_block(q_rows, second_k, second_v))
    return (state[2] / state[1][:, None]).astype(jnp.bfloat16)


def attend_item(args):
    q_head, first_k, first_v, second_k, second_v = args
    length, width = q_head.shape
    rows = min(512, length)

    def block(q_rows):
        return attend_rows(q_rows, first_k, first_v, second_k, second_v)

    return lax.map(block, q_head.reshape(length // rows, rows, width)).reshape(length, width)


def items_first(array):
    return jnp.transpose(array.reshape(array.shape[0], array.shape[2], array.shape[3]), (1, 0, 2))


def attend_items(pieces):
    q_group, k_group, v_group = pieces
    q_heads = items_first(q_group)
    k_heads = items_first(k_group)
    v_heads = items_first(v_group)
    stacked = jnp.stack([k_heads, v_heads])
    other = partner(stacked, "blk", 0)
    tiles = (q_heads, k_heads, v_heads, other[0], other[1])
    outcome = lax.map(attend_item, tiles)
    count, length, width = outcome.shape
    outcome = jnp.transpose(outcome, (1, 0, 2)).reshape(length, 1, count, width)
    return lax.all_to_all(outcome, "seq", split_axis=0, concat_axis=1, tiled=True)


def on_device(query, keys, values):
    groups = lax.axis_size("seq")
    width = query.shape[1] // HEADS
    tok_rows = query.shape[0]
    key_source, value_source = (keys, values)
    per_dev = (HEADS + groups - 1) // groups
    slots_all = per_dev * groups

    def split_heads(array):
        count_rows = array.shape[0]
        shaped = array.reshape(count_rows, HEADS, width)
        shaped = jnp.pad(shaped, ((0, 0), (0, slots_all - HEADS), (0, 0)))
        return shaped.reshape(count_rows, groups, per_dev, width)

    result = attend_items(
        (
            lax.all_to_all(split_heads(query), "seq", split_axis=1, concat_axis=0, tiled=True),
            lax.all_to_all(split_heads(key_source), "seq", split_axis=1, concat_axis=0, tiled=True),
            lax.all_to_all(
                split_heads(value_source), "seq", split_axis=1, concat_axis=0, tiled=True
            ),
        )
    )
    result = result.reshape(tok_rows, slots_all, width)[:, :HEADS]
    return result.reshape(tok_rows, HEADS * width)


def solution(mesh):
    placed = (P(("blk", "seq"), None), P(("blk", "seq"), None), P(("blk", "seq"), None))
    return jax.shard_map(
        on_device, mesh=mesh, in_specs=placed, out_specs=P(("blk", "seq"), None), check_vma=False
    )
```

profile of v0, /device:TPU:0, one launch (start us, length us, event | category | flops | bytes accessed | tf_op | source)
XLA Modules:
  0.0 155.3 jit_solution(6471587082868300585)
XLA Ops:
  0.0 1.1 copy-done
  1.3 1.0 pad.11.clone
  2.2 8.3 %all-to-all-start.1 = ((bf16[64,16,3,128]{3,0,2,1:T(8,128)(2,1)}), bf16[64,16,3,128]{3,0,2,1:T(8,128)(2,1)S(1)}, u32[]{:S(2)}, u32[]{:S(2)}) async-start(bf16[64,16,3,128]{3,0,2,1:T(8,128)(2,1)} %bitcast.13), calls=%async_computation.1 | async-start | bytes 1572864 | tf_op jit(solution)/shard_map/all_to_all | solution.py:87
  10.8 1.0 pad.12.clone
  11.8 18.5 %all-to-all-done.1 = bf16[64,16,3,128]{3,0,2,1:T(8,128)(2,1)S(1)} async-done(((bf16[64,16,3,128]{3,0,2,1:T(8,128)(2,1)}), bf16[64,16,3,128]{3,0,2,1:T(8,128)(2,1)S(1)}, u32[]{:S(2)}, u32[]{:S(2)}) %all-to-all-start.1) | async-done | bytes 786464 | tf_op jit(solution)/shard_map/all_to_all | solution.py:87
  30.3 5.0 %all-to-all-start.2 = ((bf16[64,16,3,128]{3,0,2,1:T(8,128)(2,1)}), bf16[64,16,3,128]{3,0,2,1:T(8,128)(2,1)S(1)}, u32[]{:S(2)}, u32[]{:S(2)}) async-start(bf16[64,16,3,128]{3,0,2,1:T(8,128)(2,1)} %bitcast.18), calls=%async_computation.2 | async-start | bytes 1572864 | tf_op jit(solution)/shard_map/all_to_all | solution.py:88
  35.3 18.6 %all-to-all-done.2 = bf16[64,16,3,128]{3,0,2,1:T(8,128)(2,1)S(1)} async-done(((bf16[64,16,3,128]{3,0,2,1:T(8,128)(2,1)}), bf16[64,16,3,128]{3,0,2,1:T(8,128)(2,1)S(1)}, u32[]{:S(2)}, u32[]{:S(2)}) %all-to-all-start.2) | async-done | bytes 786464 | tf_op jit(solution)/shard_map/all_to_all | solution.py:88
  53.9 0.9 copy-done.2
  54.8 1.3 copy.18
  56.0 1.3 pad_maximum_fusion
  57.5 1.0 pad.10.clone
  58.5 5.0 %all-to-all-start = ((bf16[64,16,3,128]{3,0,2,1:T(8,128)(2,1)}), bf16[64,16,3,128]{3,0,2,1:T(8,128)(2,1)S(1)}, u32[]{:S(2)}, u32[]{:S(2)}) async-start(bf16[64,16,3,128]{3,0,2,1:T(8,128)(2,1)} %bitcast.121), calls=%async_computation | async-start | bytes 1572864 | tf_op jit(solution)/shard_map/all_to_all | solution.py:86
  63.4 20.1 %all-to-all-done = bf16[64,16,3,128]{3,0,2,1:T(8,128)(2,1)S(1)} async-done(((bf16[64,16,3,128]{3,0,2,1:T(8,128)(2,1)}), bf16[64,16,3,128]{3,0,2,1:T(8,128)(2,1)S(1)}, u32[]{:S(2)}, u32[]{:S(2)}) %all-to-all-start) | async-done | bytes 786464 | tf_op jit(solution)/shard_map/all_to_all | solution.py:86
  83.5 0.9 copy.14
  84.5 2.6 %slice_bitcast_fusion = (bf16[3,1024,128]{2,1,0:T(8,128)(2,1)}, bf16[3,1024,128]{2,1,0:T(8,128)(2,1)}) fusion(bf16[2,3,1024,128]{3,2,1,0:T(8,128)(2,1)} %collective-permute-done), kind=kLoop, calls=%fused_computation.42 | loop fusion | bytes 3145728 | tf_op jit(solution)/shard_map/squeeze | solution.py:63
  87.1 34.5 %while.21 = (s32[]{:T(128)}, bf16[3,1024,128]{2,1,0:T(8,128)(2,1)}, bf16[3,1024,128]{2,1,0:T(8,128)(2,1)}, bf16[3,1024,128]{2,1,0:T(8,128)(2,1)S(1)}, bf16[3,102...) while((s32[]{:T(128)}, bf16[3,1024,128]{2,1,0:T(8,128)(2,1)}, ...), condition=%wide.region_7.8_spmd, body=%wide.region_0.7_spmd.sunk | while | flops 545588224 | bytes 18780980 | solution.py:64
  87.1 1.0 dynamic-slice_bitcast_fusion.6
  88.1 1.7 %dynamic-slice_bitcast_fusion.7 = (bf16[1024,128]{1,0:T(8,128)(2,1)}, bf16[1024,128]{1,0:T(8,128)(2,1)S(1)}) fusion(bf16[3,1024,128]{2,1,0:T(8,128)(2,1)} %get-tuple-element.302, s32[]{:T(128)} %get-tuple-element.286, bf16[3,1024,128]{2,1,0:T(8,128)(2,1)S(1)} %get-tuple-element.300), kind=kLoop, calls=%fused_computation.35.clone.1 | loop fusion | bytes 1048580 | tf_op jit(solution)/shard_map/while/body/jit(dynamic_index_in_dim)/squeeze | solution.py:64
  89.8 1.0 constant_dynamic-slice_fusion.2
  90.8 7.1 %while.22 = (s32[]{:T(128)}, bf16[2,512,128]{2,1,0:T(8,128)(2,1)S(1)}, bf16[2,512,128]{2,1,0:T(8,128)(2,1)S(1)}, bf16[1024,128]{1,0:T(8,128)(2,1)S(1)}, bf16[102...) while((s32[]{:T(128)}, ...), condition=%wide.region_6.6_spmd, body=%wide.region_1.5_spmd.sunk | while | flops 545588224 | bytes 15634557 | solution.py:49
  91.8 1.0 fusion.50
  92.8 0.5 convolution_multiply_fusion.3
  93.7 0.6 fusion.51
  95.4 1.0 fusion.50
  96.4 0.5 convolution_multiply_fusion.3
  97.3 0.6 fusion.51
  97.9 0.7 bitcast_dynamic-update-slice_fusion.2
  98.6 1.0 dynamic-slice_bitcast_fusion.6
  99.6 1.7 %dynamic-slice_bitcast_fusion.7 = (bf16[1024,128]{1,0:T(8,128)(2,1)}, bf16[1024,128]{1,0:T(8,128)(2,1)S(1)}) fusion(bf16[3,1024,128]{2,1,0:T(8,128)(2,1)} %get-tuple-element.302, s32[]{:T(128)} %get-tuple-element.286, bf16[3,1024,128]{2,1,0:T(8,128)(2,1)S(1)} %get-tuple-element.300), kind=kLoop, calls=%fused_computation.35.clone.1 | loop fusion | bytes 1048580 | tf_op jit(solution)/shard_map/while/body/jit(dynamic_index_in_dim)/squeeze | solution.py:64
  101.3 1.0 constant_dynamic-slice_fusion.2
  102.3 7.1 %while.22 = (s32[]{:T(128)}, bf16[2,512,128]{2,1,0:T(8,128)(2,1)S(1)}, bf16[2,512,128]{2,1,0:T(8,128)(2,1)S(1)}, bf16[1024,128]{1,0:T(8,128)(2,1)S(1)}, bf16[102...) while((s32[]{:T(128)}, ...), condition=%wide.region_6.6_spmd, body=%wide.region_1.5_spmd.sunk | while | flops 545588224 | bytes 15634557 | solution.py:49
  103.3 1.0 fusion.50
  105.2 0.6 fusion.51
  106.9 1.0 fusion.50
  108.8 0.6 fusion.51
  109.4 0.7 bitcast_dynamic-update-slice_fusion.2
  110.1 1.0 dynamic-slice_bitcast_fusion.6
  111.1 1.7 %dynamic-slice_bitcast_fusion.7 = (bf16[1024,128]{1,0:T(8,128)(2,1)}, bf16[1024,128]{1,0:T(8,128)(2,1)S(1)}) fusion(bf16[3,1024,128]{2,1,0:T(8,128)(2,1)} %get-tuple-element.302, s32[]{:T(128)} %get-tuple-element.286, bf16[3,1024,128]{2,1,0:T(8,128)(2,1)S(1)} %get-tuple-element.300), kind=kLoop, calls=%fused_computation.35.clone.1 | loop fusion | bytes 1048580 | tf_op jit(solution)/shard_map/while/body/jit(dynamic_index_in_dim)/squeeze | solution.py:64
  112.8 1.0 constant_dynamic-slice_fusion.2
  113.8 7.1 %while.22 = (s32[]{:T(128)}, bf16[2,512,128]{2,1,0:T(8,128)(2,1)S(1)}, bf16[2,512,128]{2,1,0:T(8,128)(2,1)S(1)}, bf16[1024,128]{1,0:T(8,128)(2,1)S(1)}, bf16[102...) while((s32[]{:T(128)}, ...), condition=%wide.region_6.6_spmd, body=%wide.region_1.5_spmd.sunk | while | flops 545588224 | bytes 15634557 | solution.py:49
  114.8 1.0 fusion.50
  116.7 0.6 fusion.51
  118.4 1.0 fusion.50
  120.3 0.6 fusion.51
  120.9 0.7 bitcast_dynamic-update-slice_fusion.2
  121.6 1.8 %copy.35 = bf16[3,1024,128]{2,0,1:T(4,128)(2,1)S(1)} copy(bf16[3,1024,128]{2,1,0:T(8,128)(2,1)} %get-tuple-element.79) | data formatting | bytes 1572864 | tf_op jit(solution)/shard_map/while | solution.py:64
  123.4 30.8 %all_to_all.60 = bf16[1024,1,3,128]{3,2,1,0:T(4,128)(2,1)S(1)} all-to-all(bf16[1024,1,3,128]{3,2,1,0:T(4,128)(2,1)S(1)} %bitcast.116), channel_id=1, replica_groups=mesh['seq'=16,'blk'=2] {'seq'}, dimensions={0} | all-to-all | bytes 1572864 | tf_op jit(solution)/shard_map/all_to_all | solution.py:67
  154.4 0.9 copy_bitcast_fusion.1
  (52 shorter events, 11.6 us)
Async XLA Ops:
  0.0 1.1 copy-start
  0.0 10.6 %copy-start.3 = (bf16[64,5120]{1,0:T(8,128)(2,1)S(1)}, bf16[64,5120]{1,0:T(8,128)(2,1)}, u32[]{:S(2)}) copy-start(bf16[64,5120]{1,0:T(8,128)(2,1)} %param.9) | copy-start | bytes 1966084
  2.2 28.0 %all-to-all-start.1 = ((bf16[64,16,3,128]{3,0,2,1:T(8,128)(2,1)}), bf16[64,16,3,128]{3,0,2,1:T(8,128)(2,1)S(1)}, u32[]{:S(2)}, u32[]{:S(2)}) async-start(bf16[64,16,3,128]{3,0,2,1:T(8,128)(2,1)} %bitcast.13), calls=%async_computation.1 | async-start | bytes 1572864 | tf_op jit(solution)/shard_map/all_to_all | solution.py:87
  30.3 23.6 %all-to-all-start.2 = ((bf16[64,16,3,128]{3,0,2,1:T(8,128)(2,1)}), bf16[64,16,3,128]{3,0,2,1:T(8,128)(2,1)S(1)}, u32[]{:S(2)}, u32[]{:S(2)}) async-start(bf16[64,16,3,128]{3,0,2,1:T(8,128)(2,1)} %bitcast.18), calls=%async_computation.2 | async-start | bytes 1572864 | tf_op jit(solution)/shard_map/all_to_all | solution.py:88
  53.9 0.9 copy-start.2
  54.8 2.6 %copy-start.4 = (bf16[64,5120]{1,0:T(8,128)(2,1)S(1)}, bf16[64,5120]{1,0:T(8,128)(2,1)}, u32[]{:S(2)}) copy-start(bf16[64,5120]{1,0:T(8,128)(2,1)} %param.7) | copy-start | bytes 1966084
  57.3 27.2 %collective-permute-start = (bf16[2,3,1024,128]{3,2,1,0:T(8,128)(2,1)}, bf16[2,3,1024,128]{3,2,1,0:T(8,128)(2,1)}, u32[]{:S(2)}, u32[]{:S(2)}) collective-permute-start(bf16[2,3,1024,128]{3,2,1,0:T(8,128)(2,1)} %pad_maximum_fusion), channel_id=1, source_target_pairs={{0,1},{1,0},{2,3},{3,2},{4,5},{5,4},{6,7},{7,6},{8,9},{9,8},{10,11... | collective-permute-start | bytes 4718600 | tf_op jit(solution)/shard_map/ppermute | solution.py:12
  58.5 25.1 %all-to-all-start = ((bf16[64,16,3,128]{3,0,2,1:T(8,128)(2,1)}), bf16[64,16,3,128]{3,0,2,1:T(8,128)(2,1)S(1)}, u32[]{:S(2)}, u32[]{:S(2)}) async-start(bf16[64,16,3,128]{3,0,2,1:T(8,128)(2,1)} %bitcast.121), calls=%async_computation | async-start | bytes 1572864 | tf_op jit(solution)/shard_map/all_to_all | solution.py:86
  92.8 1.0 copy-start.1
  96.3 1.0 copy-start.1
  104.3 1.0 copy-start.1
  107.8 1.0 copy-start.1
  115.8 1.0 copy-start.1
  119.3 1.0 copy-start.1
where the time goes:
time: 156 us; the launch traced here: 155 us
  waiting for transfers between devices  57.1 us (37%)
  blocking collectives  30.8 us (20%)
  local copies, waits for them, and re-layouts  28.7 us (18%)
  starting transfers between devices  18.2 us (12%)
  matrix products  12.9 us (8%)
  other arithmetic  7.11 us (5%)
    all_to_all x1, blocking collectives, attend_items(): lax.all_to_all(outcome, 'seq', split_axis=0, concat_axis=1, tiled=True)  30.8 us
    all_to_all x1, waiting for transfers between devices, on_device(): lax.all_to_all(split_heads(query), 'seq', split_axis=1, concat_axis=0, ti...  20.1 us
    all_to_all x1, waiting for transfers between devices, on_device(): lax.all_to_all(split_heads(value_source), 'seq', split_axis=1, concat_axi...  18.6 us
    all_to_all x1, waiting for transfers between devices, on_device(): lax.all_to_all(split_heads(key_source), 'seq', split_axis=1, concat_axis=...  18.5 us
    all_to_all x1, starting transfers between devices, on_device(): lax.all_to_all(split_heads(key_source), 'seq', split_axis=1, concat_axis=...  8.34 us
    squeeze x6, local copies, waits for them, and re-layouts, attend_items(): outcome = lax.map(attend_item, tiles)  8.03 us
    dot_general x12, matrix products, partial_block(): jnp.dot(expo.astype(jnp.bfloat16), v_tile, preferred_element_type=jnp.flo...  6.67 us
    dot_general x12, matrix products, partial_block(): lax.dot_general(q_rows, k_tile, (((1,), (1,)), ((), ())), preferred_eleme...  6.23 us
  transfers between devices with their start and end apart: 4, of which 3 were waited for; matrix products, arithmetic and copies ran while one was open for 2% of the time, Pallas kernels for 0%

commit v1 on v0

--- a/solution.py
+++ b/solution.py
@@ -1,9 +1,22 @@
+import functools
 import jax
 import jax.numpy as jnp
 from jax import lax
 from jax.sharding import PartitionSpec as P
 
 HEADS = 40
+
+
+def remake_the_blocks(arr, on_dim, dim_k):
+    f_now = lax.axis_size("seq")
+    everything = jnp.split(arr, f_now, axis=on_dim)
+    u1 = jnp.stack(everything, axis=0)
+    v_now = lax.all_to_all(u1, axis_name="seq", concat_axis=0, split_axis=0)
+    last = jnp.concatenate(v_now, axis=dim_k)
+    return last
+
+
+search_matrix_up = functools.partial(remake_the_blocks, on_dim=1, dim_k=0)
 
 
 def partner(value, axis, bit):
@@ -83,7 +96,7 @@
 
     result = attend_items(
         (
-            lax.all_to_all(split_heads(query), "seq", split_axis=1, concat_axis=0, tiled=True),
+            search_matrix_up(split_heads(query)),
             lax.all_to_all(split_heads(key_source), "seq", split_axis=1, concat_axis=0, tiled=True),
             lax.all_to_all(
                 split_heads(value_source), "seq", split_axis=1, concat_axis=0, tiled=True

time: 156 us -> 155 us (level)
  waiting for transfers between devices: 57.1 us -> 47.5 us
  local copies, waits for them, and re-layouts: 28.7 us -> 36.5 us
    unnamed x11 -> x25, local copies, waits for them, and re-layouts: 2.49 us -> 10.8 us
    all_to_all x1, waiting for transfers between devices: 18.5 us -> 13.2 us  [on_device(): lax.all_to_all(split_heads(key_source), 'seq', split_axis=1, concat_axis=...]
    all_to_all x1, waiting for transfers between devices: 18.6 us -> 14.2 us  [on_device(): lax.all_to_all(split_heads(value_source), 'seq', split_axis=1, concat_axi...]
  transfers between devices with their start and end apart: 4 -> 4, of which waited for: 3 -> 3; matrix products, arithmetic and copies ran while one was open for 2% -> 9% of each run, Pallas kernels for 0% -> 0%
where the time goes in v1:
time: 155 us; the launch traced here: 154 us
  waiting for transfers between devices  47.5 us (31%)
  local copies, waits for them, and re-layouts  36.5 us (24%)
  blocking collectives  30.8 us (20%)
  starting transfers between devices  18.4 us (12%)
  matrix products  12.9 us (8%)
  other arithmetic  7.17 us (5%)
    all_to_all x1, blocking collectives, attend_items(): lax.all_to_all(outcome, 'seq', split_axis=0, concat_axis=1, tiled=True)  30.8 us
    all_to_all x1, waiting for transfers between devices, remake_the_blocks(): v_now = lax.all_to_all(u1, axis_name='seq', concat_axis=0, split_axis=0)  20.1 us
    all_to_all x1, waiting for transfers between devices, on_device(): lax.all_to_all(split_heads(value_source), 'seq', split_axis=1, concat_axi...  14.2 us
    all_to_all x1, waiting for transfers between devices, on_device(): lax.all_to_all(split_heads(key_source), 'seq', split_axis=1, concat_axis=...  13.2 us
    unnamed x25, local copies, waits for them, and re-layouts  10.8 us
    all_to_all x1, starting transfers between devices, on_device(): lax.all_to_all(split_heads(key_source), 'seq', split_axis=1, concat_axis=...  8.47 us
    squeeze x6, local copies, waits for them, and re-layouts, attend_items(): outcome = lax.map(attend_item, tiles)  8.03 us
    dot_general x12, matrix products, partial_block(): jnp.dot(expo.astype(jnp.bfloat16), v_tile, preferred_element_type=jnp.flo...  6.67 us
  transfers between devices with their start and end apart: 4, of which 3 were waited for; matrix products, arithmetic and copies ran while one was open for 9% of the time, Pallas kernels for 0%

profile of v1, /device:TPU:0, one launch (start us, length us, event | category | flops | bytes accessed | tf_op | source)
XLA Modules:
  0.0 153.7 jit_solution(8396472320951399135)
XLA Ops:
  0.0 1.1 copy-done
  1.3 1.0 pad.11.clone
  2.2 8.5 %all-to-all-start.1 = ((bf16[64,16,3,128]{3,0,2,1:T(8,128)(2,1)}), bf16[64,16,3,128]{3,0,2,1:T(8,128)(2,1)S(1)}, u32[]{:S(2)}, u32[]{:S(2)}) async-start(bf16[64,16,3,128]{3,0,2,1:T(8,128)(2,1)} %bitcast.27), calls=%async_computation.1 | async-start | bytes 1572864 | tf_op jit(solution)/shard_map/all_to_all | solution.py:100
  11.0 0.7 fusion.42
  11.9 1.0 pad.12.clone
  12.8 0.6 fusion.41
  13.5 0.6 fusion.40
  14.1 0.6 fusion.39
  14.7 0.6 fusion.38
  17.2 13.2 %all-to-all-done.1 = bf16[64,16,3,128]{3,0,2,1:T(8,128)(2,1)S(1)} async-done(((bf16[64,16,3,128]{3,0,2,1:T(8,128)(2,1)}), bf16[64,16,3,128]{3,0,2,1:T(8,128)(2,1)S(1)}, u32[]{:S(2)}, u32[]{:S(2)}) %all-to-all-start.1) | async-done | bytes 786464 | tf_op jit(solution)/shard_map/all_to_all | solution.py:100
  30.4 5.0 %all-to-all-start.2 = ((bf16[64,16,3,128]{3,0,2,1:T(8,128)(2,1)}), bf16[64,16,3,128]{3,0,2,1:T(8,128)(2,1)S(1)}, u32[]{:S(2)}, u32[]{:S(2)}) async-start(bf16[64,16,3,128]{3,0,2,1:T(8,128)(2,1)} %bitcast.32), calls=%async_computation.2 | async-start | bytes 1572864 | tf_op jit(solution)/shard_map/all_to_all | solution.py:101
  35.4 0.6 fusion.34
  36.6 0.6 fusion.32
  37.2 0.6 fusion.31
  37.9 0.6 fusion.30
  39.1 0.6 fusion.28
  39.8 14.2 %all-to-all-done.2 = bf16[64,16,3,128]{3,0,2,1:T(8,128)(2,1)S(1)} async-done(((bf16[64,16,3,128]{3,0,2,1:T(8,128)(2,1)}), bf16[64,16,3,128]{3,0,2,1:T(8,128)(2,1)S(1)}, u32[]{:S(2)}, u32[]{:S(2)}) %all-to-all-start.2) | async-done | bytes 786464 | tf_op jit(solution)/shard_map/all_to_all | solution.py:101
  54.1 1.3 pad_maximum_fusion
  55.4 1.4 fusion.27
  56.8 5.0 %all-to-all-start = ((bf16[16,64,1,3,128]{4,1,3,2,0:T(8,128)(2,1)}), bf16[16,64,1,3,128]{4,1,3,2,0:T(8,128)(2,1)S(1)}, u32[]{:S(2)}, u32[]{:S(2)}) async-start(bf16[16,64,1,3,128]{4,1,3,2,0:T(8,128)(2,1)} %fusion.27), calls=%async_computation | async-start | bytes 1572864 | tf_op jit(solution)/shard_map/all_to_all | solution.py:14
  61.8 20.1 %all-to-all-done = bf16[16,64,1,3,128]{4,1,3,2,0:T(8,128)(2,1)S(1)} async-done(((bf16[16,64,1,3,128]{4,1,3,2,0:T(8,128)(2,1)}), bf16[16,64,1,3,128]{4,1,3,2,0:T(8,128)(2,1)S(1)}, u32[]{:S(2)}, u32[]{:S(2)}) %all-to-all-start) | async-done | bytes 786464 | tf_op jit(solution)/shard_map/all_to_all | solution.py:14
  81.9 1.0 copy.69
  82.8 2.6 %slice_bitcast_fusion = (bf16[3,1024,128]{2,1,0:T(8,128)(2,1)}, bf16[3,1024,128]{2,1,0:T(8,128)(2,1)}) fusion(bf16[2,3,1024,128]{3,2,1,0:T(8,128)(2,1)} %collective-permute-done), kind=kLoop, calls=%fused_computation.42 | loop fusion | bytes 3145728 | tf_op jit(solution)/shard_map/squeeze | solution.py:76
  85.5 34.6 %while.21 = (s32[]{:T(128)}, bf16[3,1024,128]{2,1,0:T(8,128)(2,1)}, bf16[3,1024,128]{2,1,0:T(8,128)(2,1)}, bf16[3,1024,128]{2,1,0:T(8,128)(2,1)S(1)}, bf16[3,102...) while((s32[]{:T(128)}, bf16[3,1024,128]{2,1,0:T(8,128)(2,1)}, ...), condition=%wide.region_7.8_spmd, body=%wide.region_0.7_spmd.sunk | while | flops 545588224 | bytes 18780980 | solution.py:77
  85.5 1.0 dynamic-slice_bitcast_fusion.6
  86.4 1.7 %dynamic-slice_bitcast_fusion.7 = (bf16[1024,128]{1,0:T(8,128)(2,1)}, bf16[1024,128]{1,0:T(8,128)(2,1)S(1)}) fusion(bf16[3,1024,128]{2,1,0:T(8,128)(2,1)} %get-tuple-element.302, s32[]{:T(128)} %get-tuple-element.286, bf16[3,1024,128]{2,1,0:T(8,128)(2,1)S(1)} %get-tuple-element.300), kind=kLoop, calls=%fused_computation.35.clone.1 | loop fusion | bytes 1048580 | tf_op jit(solution)/shard_map/while/body/jit(dynamic_index_in_dim)/squeeze | solution.py:77
  88.1 1.0 constant_dynamic-slice_fusion.2
  89.1 7.1 %while.22 = (s32[]{:T(128)}, bf16[2,512,128]{2,1,0:T(8,128)(2,1)S(1)}, bf16[2,512,128]{2,1,0:T(8,128)(2,1)S(1)}, bf16[1024,128]{1,0:T(8,128)(2,1)S(1)}, bf16[102...) while((s32[]{:T(128)}, ...), condition=%wide.region_6.6_spmd, body=%wide.region_1.5_spmd.sunk | while | flops 545588224 | bytes 15634557 | solution.py:62
  90.2 1.0 fusion.66
  93.7 1.0 fusion.66
  96.3 0.7 bitcast_dynamic-update-slice_fusion.2
  97.0 1.0 dynamic-slice_bitcast_fusion.6
  98.0 1.7 %dynamic-slice_bitcast_fusion.7 = (bf16[1024,128]{1,0:T(8,128)(2,1)}, bf16[1024,128]{1,0:T(8,128)(2,1)S(1)}) fusion(bf16[3,1024,128]{2,1,0:T(8,128)(2,1)} %get-tuple-element.302, s32[]{:T(128)} %get-tuple-element.286, bf16[3,1024,128]{2,1,0:T(8,128)(2,1)S(1)} %get-tuple-element.300), kind=kLoop, calls=%fused_computation.35.clone.1 | loop fusion | bytes 1048580 | tf_op jit(solution)/shard_map/while/body/jit(dynamic_index_in_dim)/squeeze | solution.py:77
  99.7 1.0 constant_dynamic-slice_fusion.2
  100.6 7.1 %while.22 = (s32[]{:T(128)}, bf16[2,512,128]{2,1,0:T(8,128)(2,1)S(1)}, bf16[2,512,128]{2,1,0:T(8,128)(2,1)S(1)}, bf16[1024,128]{1,0:T(8,128)(2,1)S(1)}, bf16[102...) while((s32[]{:T(128)}, ...), condition=%wide.region_6.6_spmd, body=%wide.region_1.5_spmd.sunk | while | flops 545588224 | bytes 15634557 | solution.py:62
  101.7 1.0 fusion.66
  105.2 1.0 fusion.66
  107.8 0.7 bitcast_dynamic-update-slice_fusion.2
  108.5 1.0 dynamic-slice_bitcast_fusion.6
  109.5 1.7 %dynamic-slice_bitcast_fusion.7 = (bf16[1024,128]{1,0:T(8,128)(2,1)}, bf16[1024,128]{1,0:T(8,128)(2,1)S(1)}) fusion(bf16[3,1024,128]{2,1,0:T(8,128)(2,1)} %get-tuple-element.302, s32[]{:T(128)} %get-tuple-element.286, bf16[3,1024,128]{2,1,0:T(8,128)(2,1)S(1)} %get-tuple-element.300), kind=kLoop, calls=%fused_computation.35.clone.1 | loop fusion | bytes 1048580 | tf_op jit(solution)/shard_map/while/body/jit(dynamic_index_in_dim)/squeeze | solution.py:77
  111.2 1.0 constant_dynamic-slice_fusion.2
  112.1 7.1 %while.22 = (s32[]{:T(128)}, bf16[2,512,128]{2,1,0:T(8,128)(2,1)S(1)}, bf16[2,512,128]{2,1,0:T(8,128)(2,1)S(1)}, bf16[1024,128]{1,0:T(8,128)(2,1)S(1)}, bf16[102...) while((s32[]{:T(128)}, ...), condition=%wide.region_6.6_spmd, body=%wide.region_1.5_spmd.sunk | while | flops 545588224 | bytes 15634557 | solution.py:62
  113.2 1.0 fusion.66
  116.8 1.0 fusion.66
  119.3 0.7 bitcast_dynamic-update-slice_fusion.2
  120.0 1.8 %copy.89 = bf16[3,1024,128]{2,0,1:T(4,128)(2,1)S(1)} copy(bf16[3,1024,128]{2,1,0:T(8,128)(2,1)} %get-tuple-element.79) | data formatting | bytes 1572864 | tf_op jit(solution)/shard_map/while | solution.py:77
  121.8 30.8 %all_to_all.50 = bf16[1024,1,3,128]{3,2,1,0:T(4,128)(2,1)S(1)} all-to-all(bf16[1024,1,3,128]{3,2,1,0:T(4,128)(2,1)S(1)} %bitcast.177), channel_id=1, replica_groups=mesh['seq'=16,'blk'=2] {'seq'}, dimensions={0} | all-to-all | bytes 1572864 | tf_op jit(solution)/shard_map/all_to_all | solution.py:80
  152.8 0.9 copy_bitcast_fusion.1
  (68 shorter events, 19.4 us)
Async XLA Ops:
  0.0 1.1 copy-start
  0.0 10.7 %copy-start.3 = (bf16[64,5120]{1,0:T(8,128)(2,1)S(1)}, bf16[64,5120]{1,0:T(8,128)(2,1)}, u32[]{:S(2)}) copy-start(bf16[64,5120]{1,0:T(8,128)(2,1)} %param.7) | copy-start | bytes 1966084
  2.2 9.4 %copy-start.4 = (bf16[64,5120]{1,0:T(8,128)(2,1)S(1)}, bf16[64,5120]{1,0:T(8,128)(2,1)}, u32[]{:S(2)}) copy-start(bf16[64,5120]{1,0:T(8,128)(2,1)} %param.9) | copy-start | bytes 1966084
  2.2 28.2 %all-to-all-start.1 = ((bf16[64,16,3,128]{3,0,2,1:T(8,128)(2,1)}), bf16[64,16,3,128]{3,0,2,1:T(8,128)(2,1)S(1)}, u32[]{:S(2)}, u32[]{:S(2)}) async-start(bf16[64,16,3,128]{3,0,2,1:T(8,128)(2,1)} %bitcast.27), calls=%async_computation.1 | async-start | bytes 1572864 | tf_op jit(solution)/shard_map/all_to_all | solution.py:100
  11.0 28.1 %copy-start.2 = (bf16[64,48,128]{2,0,1:T(8,128)(2,1)}, bf16[64,48,128]{2,0,1:T(8,128)(2,1)S(1)}, u32[]{:S(2)}) copy-start(bf16[64,48,128]{2,0,1:T(8,128)(2,1)S(1)} %pad.10) | copy-start | bytes 2359300
  30.4 23.6 %all-to-all-start.2 = ((bf16[64,16,3,128]{3,0,2,1:T(8,128)(2,1)}), bf16[64,16,3,128]{3,0,2,1:T(8,128)(2,1)S(1)}, u32[]{:S(2)}, u32[]{:S(2)}) async-start(bf16[64,16,3,128]{3,0,2,1:T(8,128)(2,1)} %bitcast.32), calls=%async_computation.2 | async-start | bytes 1572864 | tf_op jit(solution)/shard_map/all_to_all | solution.py:101
  55.4 27.5 %collective-permute-start = (bf16[2,3,1024,128]{3,2,1,0:T(8,128)(2,1)}, bf16[2,3,1024,128]{3,2,1,0:T(8,128)(2,1)}, u32[]{:S(2)}, u32[]{:S(2)}) collective-permute-start(bf16[2,3,1024,128]{3,2,1,0:T(8,128)(2,1)} %pad_maximum_fusion), channel_id=1, source_target_pairs={{0,1},{1,0},{2,3},{3,2},{4,5},{5,4},{6,7},{7,6},{8,9},{9,8},{10,11... | collective-permute-start | bytes 4718600 | tf_op jit(solution)/shard_map/ppermute | solution.py:25
  56.8 25.1 %all-to-all-start = ((bf16[16,64,1,3,128]{4,1,3,2,0:T(8,128)(2,1)}), bf16[16,64,1,3,128]{4,1,3,2,0:T(8,128)(2,1)S(1)}, u32[]{:S(2)}, u32[]{:S(2)}) async-start(bf16[16,64,1,3,128]{4,1,3,2,0:T(8,128)(2,1)} %fusion.27), calls=%async_computation | async-start | bytes 1572864 | tf_op jit(solution)/shard_map/all_to_all | solution.py:14
  91.1 1.0 copy-start.1
  94.7 1.0 copy-start.1
  102.6 1.0 copy-start.1
  106.2 1.0 copy-start.1
  114.2 1.0 copy-start.1
  117.7 1.0 copy-start.1
